TPU v7x, 32 devices: a whole 2x2x4 slice. The times are simulated.
32 devices in a mesh: rows: 4 (over y, x), feat: 8 (over z, core).
Axes of the slice: x: 2, y: 2, z: 4, core: 2. Of those that a mesh axis runs over, the one named last changes fastest.
Arguments:
- bins: int32 [256, 32768], P(None, ('rows', 'feat')), may hold values from 0 to 255
- leaf: int32 [32768], P(('rows', 'feat')), may hold values from 0 to 1
- grad: bfloat16 [32, 32768], P(None, ('rows', 'feat')), may hold values from -15.55 to 15.55
- hess: bfloat16 [32, 32768], P(None, ('rows', 'feat')), may hold values from 0.049804688 to 1
Outputs:
- gains: float32 [256, 2, 256], P(('rows', 'feat'))
- best: float32 [2], replicated
All inputs are finite; a program needn't handle non-finite values.
Results may differ from a plain program's by a relative error of at most 0.0003.
Values may be sent and summed in bfloat16 or wider, within the bound.
A program may use at most 128 MiB of HBM per device.

v0:
```python
import math

import jax
import jax.numpy as jnp
from jax import lax
from jax.sharding import PartitionSpec as P

F = 256
B = 256
LEAVES = 2


def leaf_weighted(both, leaf_row, leaves):
    nodes = jnp.arange(leaves, dtype=jnp.float32)[:, None]
    hot = (leaf_row.astype(jnp.float32) == nodes).astype(jnp.bfloat16)
    return (hot[:, None, :] * both[None, :, :]).reshape(leaves * both.shape[0], both.shape[1])


def bin_counts(codes, weighted, bin_total):
    levels = jnp.arange(bin_total, dtype=jnp.int32)
    onehot = (codes[:, :, None] == levels).astype(jnp.bfloat16)
    return jnp.einsum("frb,cr->fbc", onehot, weighted, preferred_element_type=jnp.float32)


def split_gains(hist, totals, outputs):
    count = hist.shape[0]
    cum = jnp.cumsum(hist, axis=1).reshape(count, B, LEAVES, 2, outputs)
    tot = totals.reshape(LEAVES, 2, outputs)
    left_grad = cum[:, :, :, 0, :]
    left_hess = cum[:, :, :, 1, :]
    all_grad = tot[:, 0, :]
    all_hess = tot[:, 1, :]
    right_grad = all_grad - left_grad
    right_hess = all_hess - left_hess
    score = (
        left_grad * left_grad / (left_hess + 1.0)
        + right_grad * right_grad / (right_hess + 1.0)
        - all_grad * all_grad / (all_hess + 1.0)
    )
    gains = 0.5 / outputs * jnp.sum(score, axis=-1)
    return jnp.transpose(gains, (0, 2, 1))


def shards(bins, leaf, grad, hess):
    outputs = grad.shape[0]
    shard = bins.shape[1]
    devices = lax.axis_size("rows") * lax.axis_size("feat")
    owned = F // devices
    both = jnp.concatenate([grad, hess], axis=0)
    leaf_row = leaf[None, :]
    weighted = leaf_weighted(both, leaf_row, LEAVES)
    columns = weighted.shape[0]
    codes_mine = lax.all_to_all(bins, ("rows", "feat"), split_axis=0, concat_axis=1, tiled=True)
    initial = jnp.zeros((owned, B, columns), jnp.float32)
    both_piece = lax.all_gather(both, ("rows", "feat"), axis=1, tiled=True)
    leaf_piece = lax.all_gather(leaf_row.astype(jnp.bfloat16), ("rows", "feat"), axis=1, tiled=True)
    length = both_piece.shape[1]
    width = math.gcd(length, 8 * shard)

    def step(index, total):
        offset = index * width
        part_codes = lax.dynamic_slice_in_dim(codes_mine, offset, width, 1)
        part_both = lax.dynamic_slice_in_dim(both_piece, offset, width, 1)
        part_leaf = lax.dynamic_slice_in_dim(leaf_piece, offset, width, 1)
        return total + bin_counts(part_codes, leaf_weighted(part_both, part_leaf, LEAVES), B)

    hist = lax.fori_loop(0, length // width, step, initial)
    totals = lax.psum(jnp.sum(weighted, axis=1, dtype=jnp.float32), ("rows", "feat"))
    gains = split_gains(hist, totals, outputs)
    best = lax.pmax(jnp.max(gains, axis=(0, 2)), ("rows", "feat"))
    return (gains, best)


def solution(mesh):
    return jax.shard_map(
        shards,
        mesh=mesh,
        in_specs=(
            P(None, ("rows", "feat")),
            P(("rows", "feat")),
            P(None, ("rows", "feat")),
            P(None, ("rows", "feat")),
        ),
        out_specs=(P(("rows", "feat"), None, None), P()),
        check_vma=False,
    )
```

profile of v0, /device:TPU:0, one launch (start us, length us, event | category | flops | bytes accessed | tf_op | source)
XLA Modules:
  0.0 226.1 jit_solution(3870619815995787336)
XLA Ops:
  7.2 0.0 copy-start.2
  7.2 0.0 all-gather.3.cloned.1.call-start
  7.2 0.8 constant_dynamic-update-slice_fusion.1
  8.1 0.8 constant_dynamic-update-slice_fusion
  8.9 0.0 copy-start
  8.9 0.6 copy-done
  9.5 0.0 all-gather.3.cloned.1.call-update
  9.6 0.0 copy-start.1
  9.6 7.3 %all-to-all-start = ((s32[32,8,1024]{2,1,0:T(8,128)}), s32[32,8,1024]{2,1,0:T(8,128)S(1)}, u32[]{:S(2)}, u32[]{:S(2)}) async-start(s32[32,8,1024]{2,1,0:T(8,128)} %bitcast.44), calls=%async_computation | async-start | bytes 2097152 | tf_op jit(solution)/shard_map/all_to_all | solution.py:53
  16.9 0.0 copy-done.2
  17.0 0.0 copy-done.1
  17.0 0.1 convert_reduce_fusion
  17.1 0.1 reshape.98
  17.2 60.4 %all-gather = bf16[32768]{0:T(1024)(128)(2,1)S(1)} all-gather(bf16[1024]{0:T(1024)(128)(2,1)S(1)} %get-tuple-element.128), channel_id=2, replica_groups=mesh['rows'=4,'feat'=8] {'rows','feat'}, dimensions={0}, use_global_device_ids=true | all-gather | bytes 67584 | tf_op jit(solution)/shard_map/all_gather | solution.py:56
  77.6 0.1 reshape.101
  77.6 37.5 %psum.7 = f32[2,2,32]{2,1,0:T(2,128)S(1)} all-reduce(f32[2,2,32]{2,1,0:T(2,128)S(1)} %reshape.98), channel_id=1, replica_groups=mesh['rows'=4,'feat'=8] {'rows','feat'}, use_global_device_ids=true, to_apply=%region_5.6 | all-reduce | flops 128 | bytes 1024 | tf_op jit(solution)/shard_map/psum | solution.py:68
  115.2 0.0 all-to-all-done
  115.2 0.0 all-gather.3.cloned.1.call-done
  115.2 58.8 %while.14 = (s32[]{:T(128)}, f32[8,256,128]{2,1,0:T(8,128)}, s32[8,32768]{1,0:T(8,128)S(1)}, bf16[1,32768]{1,0:T(2,128)(2,1)S(1)}, bf16[64,32768]{1,0:T(8,128)(2...) while((s32[]{:T(128)}, f32[8,256,128]{2,1,0:T(8,128)}, s32[8,32768]{1,0:T(8,128)S(1)}, ...), condition=%wide.region_1.0_spmd.clone, body=%wide.region_0.0_spmd.clone.sunk | while | flops 4313358336 | bytes 10371233 | solution.py:67
  115.2 1.3 constant_dynamic-slice_fusion.4
  116.6 0.2 broadcast_multiply_fusion.2
  116.8 12.3 %fusion.12 = f32[8,256,128]{2,1,0:T(8,128)} fusion(bf16[128,8192,1]{1,0,2:T(8,128)(2,1)S(1)} %bitcast.39, s32[8,8192]{1,0:T(8,128)S(1)} %constant_dynamic-slice_fusion.5, f32[8,256,128]{2,1,0:T(8,128)} %get-tuple-element.172, pred[]{:T(512)S(6)} %compare.3), kind=kOutput, calls=%fused_computation.3.clone.1 | convolution fusion | flops 4312268800 | bytes 4456449 | tf_op jit(solution)/shard_map/while/body/eval_jaxpr/frb,cr->fbc/dot_general | solution.py:22
  129.2 1.3 constant_dynamic-slice_fusion.4
  130.6 0.2 broadcast_multiply_fusion.2
  130.8 13.3 %fusion.12 = f32[8,256,128]{2,1,0:T(8,128)} fusion(bf16[128,8192,1]{1,0,2:T(8,128)(2,1)S(1)} %bitcast.39, s32[8,8192]{1,0:T(8,128)S(1)} %constant_dynamic-slice_fusion.5, f32[8,256,128]{2,1,0:T(8,128)} %get-tuple-element.172, pred[]{:T(512)S(6)} %compare.3), kind=kOutput, calls=%fused_computation.3.clone.1 | convolution fusion | flops 4312268800 | bytes 4456449 | tf_op jit(solution)/shard_map/while/body/eval_jaxpr/frb,cr->fbc/dot_general | solution.py:22
  144.1 1.3 constant_dynamic-slice_fusion.4
  145.5 0.2 broadcast_multiply_fusion.2
  145.7 13.4 %fusion.12 = f32[8,256,128]{2,1,0:T(8,128)} fusion(bf16[128,8192,1]{1,0,2:T(8,128)(2,1)S(1)} %bitcast.39, s32[8,8192]{1,0:T(8,128)S(1)} %constant_dynamic-slice_fusion.5, f32[8,256,128]{2,1,0:T(8,128)} %get-tuple-element.172, pred[]{:T(512)S(6)} %compare.3), kind=kOutput, calls=%fused_computation.3.clone.1 | convolution fusion | flops 4312268800 | bytes 4456449 | tf_op jit(solution)/shard_map/while/body/eval_jaxpr/frb,cr->fbc/dot_general | solution.py:22
  159.1 1.3 constant_dynamic-slice_fusion.4
  160.4 0.2 broadcast_multiply_fusion.2
  160.6 13.4 %fusion.12 = f32[8,256,128]{2,1,0:T(8,128)} fusion(bf16[128,8192,1]{1,0,2:T(8,128)(2,1)S(1)} %bitcast.39, s32[8,8192]{1,0:T(8,128)S(1)} %constant_dynamic-slice_fusion.5, f32[8,256,128]{2,1,0:T(8,128)} %get-tuple-element.172, pred[]{:T(512)S(6)} %compare.3), kind=kOutput, calls=%fused_computation.3.clone.1 | convolution fusion | flops 4312268800 | bytes 4456449 | tf_op jit(solution)/shard_map/while/body/eval_jaxpr/frb,cr->fbc/dot_general | solution.py:22
  174.0 1.8 fusion.3
  175.8 0.1 fusion.5
  175.9 0.1 broadcast_add_fusion
  176.0 0.4 copy.15
  176.4 0.4 subtract_reduce_fusion
  176.8 0.7 multiply_reduce_fusion
  177.5 41.8 %pmax.7 = f32[2]{0:T(128)} all-reduce(f32[2]{0:T(128)S(1)} %get-tuple-element.125), channel_id=1, replica_groups=mesh['rows'=4,'feat'=8] {'rows','feat'}, use_global_device_ids=true, to_apply=%region_8.9 | all-reduce | flops 2 | bytes 16 | tf_op jit(solution)/shard_map/pmax | solution.py:70
  (18 shorter events, 0.4 us)
Async XLA Ops:
  7.2 9.8 %copy-start.2 = (s32[1024]{0:T(1024)S(1)}, s32[1024]{0:T(1024)}, u32[]{:S(2)}) copy-start(s32[1024]{0:T(1024)} %param.7) | copy-start | bytes 12292
  7.2 108.0 %all-gather.3.cloned.1.call-start = ((), (), s32[]{:S(2)}) async-start(), calls=%async_computation.1 | async-start | bytes 4325376 | tf_op jit(solution)/shard_map/all_gather | solution.py:55
  8.9 0.6 copy-start
  9.6 7.4 %copy-start.1 = (bf16[64,1024]{1,0:T(8,128)(2,1)S(1)}, bf16[64,1024]{1,0:T(8,128)(2,1)}, u32[]{:S(2)}) copy-start(bf16[64,1024]{1,0:T(8,128)(2,1)} %copy-done) | copy-start | bytes 393220
  9.6 105.6 %all-to-all-start = ((s32[32,8,1024]{2,1,0:T(8,128)}), s32[32,8,1024]{2,1,0:T(8,128)S(1)}, u32[]{:S(2)}, u32[]{:S(2)}) async-start(s32[32,8,1024]{2,1,0:T(8,128)} %bitcast.44), calls=%async_computation | async-start | bytes 2097152 | tf_op jit(solution)/shard_map/all_to_all | solution.py:53
Sparse Core Ops, SparseCore 0:
  11.0 66.5 all-gather.2
where the time goes:
time: 227 us; the launch traced here: 226 us
  blocking collectives  140 us (62%)
  matrix products  52.4 us (23%)
  between operations  14.1 us (6%)
  local copies, waits for them, and re-layouts  8.17 us (4%)
  starting transfers between devices  7.37 us (3%)
  other arithmetic  4.15 us (2%)
    all_gather x1, blocking collectives, shards(): lax.all_gather(leaf_row.astype(jnp.bfloat16), ('rows', 'feat'), axis=1, t...  60.4 us
    dot_general x4, matrix products, bin_counts(): jnp.einsum('frb,cr->fbc', onehot, weighted, preferred_element_type=jnp.fl...  52.4 us
    pmax x1, blocking collectives, shards(): best = lax.pmax(jnp.max(gains, axis=(0, 2)), ('rows', 'feat'))  41.8 us
    psum x1, blocking collectives, shards(): lax.psum(jnp.sum(weighted, axis=1, dtype=jnp.float32), ('rows', 'feat'))  37.5 us
    all_to_all x1, starting transfers between devices, shards(): lax.all_to_all(bins, ('rows', 'feat'), split_axis=0, concat_axis=1, tiled...  7.33 us
    dynamic_slice x4, local copies, waits for them, and re-layouts, step(): part_both = lax.dynamic_slice_in_dim(both_piece, offset, width, 1)  5.17 us
  transfers between devices with their start and end apart: 2, of which 0 were waited for; matrix products, arithmetic and copies ran while one was open for 0% of the time, Pallas kernels for 0%

commit v1 on v0

v1 whole, which is shorter than its diff:
```python
import functools

import jax
import jax.numpy as jnp
from jax import lax
from jax.experimental import pallas as pl
from jax.experimental.pallas import tpu as pltpu
from jax.sharding import PartitionSpec as P

B = 256
LEAVES = 2
LANES = 128
MESH = pl.DeviceIdType.MESH


def add_block(codes, packed, acc_ref, outputs, shard):
    chunks = shard // LANES
    height = 2 * outputs
    both = jnp.concatenate([packed[j * height:(j + 1) * height, :] for j in range(chunks)], axis=1)
    start = chunks * height
    node = jnp.concatenate([packed[start + j:start + j + 1, :] for j in range(chunks)], axis=1)
    zero = jnp.zeros_like(both)
    weighted = jnp.concatenate([jnp.where(node == leaf, both, zero) for leaf in range(LEAVES)], axis=0)
    width = min(shard, 1024)
    levels = lax.broadcasted_iota(jnp.int32, (B, width), 0).astype(jnp.float32).astype(jnp.bfloat16)
    one = jnp.ones((B, width), jnp.bfloat16)
    none = jnp.zeros((B, width), jnp.bfloat16)
    for f in range(codes.shape[0]):
        total = acc_ref[f]
        for k in range(0, shard, width):
            upto = jnp.where(codes[f:f + 1, k:k + width] <= levels, one, none)
            total = total + lax.dot_general(
                weighted[:, k:k + width], upto, (((1,), (1,)), ((), ())), preferred_element_type=jnp.float32
            )
        acc_ref[f] = total


def feature_gains(cum, outputs):
    rows = []
    for leaf in range(LEAVES):
        base = leaf * 2 * outputs
        left_grad = cum[base:base + outputs]
        left_hess = cum[base + outputs:base + 2 * outputs]
        all_grad = left_grad[:, B - 1:B]
        all_hess = left_hess[:, B - 1:B]
        right_grad = all_grad - left_grad
        right_hess = all_hess - left_hess
        score = (
            left_grad * left_grad / (left_hess + 1.0)
            + right_grad * right_grad / (right_hess + 1.0)
            - all_grad * all_grad / (all_hess + 1.0)
        )
        rows.append(0.5 / outputs * jnp.sum(score, axis=0, keepdims=True))
    return jnp.concatenate(rows, axis=0)


def kernel(sizes, outputs, shard, owned, codes_in, packed_in, gains_ref, best_ref,
           codes_all, packed_all, acc_ref, best_all, send_c, recv_c, send_g, recv_g, send_b, recv_b):
    na, nb, nz = sizes
    pairs = na * nb * nz
    count = 2 * pairs
    r = lax.axis_index("rows")
    f = lax.axis_index("feat")
    a, b = r // nb, r % nb
    z, c = f // 2, f % 2

    def place(pa, pb, pz, pc):
        return {"rows": pa * nb + pb, "feat": pz * 2 + pc}

    def line(pa, pb, pz, pc):
        return ((pa * nb + pb) * nz + pz) * 2 + pc

    def digits(p):
        return p // (nb * nz), (p // nz) % nb, p % nz

    me = line(a, b, z, c)

    def source(p, pc):
        da, db, dz = digits(p)
        return line((a + da) % na, (b + db) % nb, (z + dz) % nz, pc)

    def target(s):
        da, db, dz = digits(s // 2)
        return (a + na - da) % na, (b + nb - db) % nb, (z + nz - dz) % nz, (c + s) % 2

    barrier = pltpu.get_barrier_semaphore()

    @pl.loop(1, count)
    def _(s):
        pl.semaphore_signal(barrier, inc=1, device_id=place(*target(s)), device_id_type=MESH)

    pl.semaphore_wait(barrier, count - 1)

    def packed_copy(src, slot, sem, where):
        return pltpu.make_async_remote_copy(
            src_ref=src, dst_ref=packed_all.at[slot], send_sem=send_g.at[sem], recv_sem=recv_g.at[slot],
            device_id=where, device_id_type=MESH)

    def codes_copy(s):
        where = target(s)
        return pltpu.make_async_remote_copy(
            src_ref=codes_in.at[line(*where)], dst_ref=codes_all.at[me], send_sem=send_c.at[s],
            recv_sem=recv_c.at[me], device_id=place(*where), device_id_type=MESH)

    def best_copy(s):
        return pltpu.make_async_remote_copy(
            src_ref=best_all.at[me], dst_ref=best_all.at[me], send_sem=send_b.at[s],
            recv_sem=recv_b.at[me], device_id=place(*target(s)), device_id_type=MESH)

    other = 1 - c
    for k in range(1, nz):
        packed_copy(packed_in, me, k, place(a, b, (z + nz - k) % nz, c)).start()
    packed_copy(packed_in, me, nz, place(a, (b + 1) % nb, z, c)).start()
    for k in range(1, na):
        packed_copy(packed_in, me, nb * nz * k, place((a + na - k) % na, b, z, c)).start()
    packed_copy(packed_in, me, nb * nz * na, place(a, b, z, other)).start()

    @pl.loop(1, count)
    def _(s):
        codes_copy(s).start()

    acc_ref[...] = jnp.zeros_like(acc_ref)
    packed_all[me] = packed_in[...]
    codes_all[me] = codes_in[me]

    @pl.loop(0, count)
    def _(s):
        p = s // 2
        here = source(p, (c + s) % 2)

        @pl.when(s > 0)
        def _():
            codes_copy_wait = pltpu.make_async_remote_copy(
                src_ref=codes_all.at[here], dst_ref=codes_all.at[here], send_sem=send_c.at[0],
                recv_sem=recv_c.at[here], device_id=place(a, b, z, other), device_id_type=MESH)
            codes_copy_wait.wait_recv()

        @pl.when(s % 2 == 1)
        def _():
            packed_copy(packed_in, here, 0, place(a, b, z, other)).wait_recv()

        add_block(codes_all[here], packed_all[here], acc_ref, outputs, shard)

        @pl.when(jnp.logical_and(s % 2 == 0, s + 2 < count))
        def _():
            q = p + 1
            slot = source(q, c)
            block = packed_all.at[slot]
            packed_copy(packed_in, slot, 0, place(a, b, z, other)).wait_recv()

            @pl.when(q < nb * nz)
            def _():
                for k in range(1, na):
                    packed_copy(block, slot, nb * nz * k + q, place((a + na - k) % na, b, z, c)).start()

            @pl.when(q < nz)
            def _():
                packed_copy(block, slot, nz + q, place(a, (b + 1) % nb, z, c)).start()

            packed_copy(block, slot, nb * nz * na + q, place(a, b, z, other)).start()

    top = None
    for i in range(owned):
        value = feature_gains(acc_ref[i], outputs)
        gains_ref[i] = value
        top = value if top is None else jnp.maximum(top, value)
    peak = jnp.max(top, axis=1, keepdims=True)
    lane = lax.broadcasted_iota(jnp.int32, (1, LANES), 1)
    best_all[me] = jnp.where(lane < LANES // 2, peak[0:1], peak[1:2])

    @pl.loop(1, count)
    def _(s):
        codes_copy(s).wait_send()
        packed_copy(packed_in, me, s, place(a, b, z, other)).wait_send()

    @pl.loop(1, count)
    def _(s):
        best_copy(s).start()

    @pl.loop(1, count)
    def _(s):
        here = source(s // 2, (c + s) % 2)
        pltpu.make_async_remote_copy(
            src_ref=best_all.at[here], dst_ref=best_all.at[here], send_sem=send_b.at[0],
            recv_sem=recv_b.at[here], device_id=place(a, b, z, other), device_id_type=MESH).wait_recv()

    @pl.loop(1, count)
    def _(s):
        best_copy(s).wait_send()

    best_ref[...] = jnp.max(best_all[...], axis=0)


def shards(sizes, bins, leaf, grad, hess):
    na, nb, nz = sizes
    count = na * nb * nz * 2
    outputs = grad.shape[0]
    features, shard = bins.shape
    owned = features // count
    chunks = shard // LANES
    codes = bins.astype(jnp.bfloat16).reshape(count, owned, shard)
    both = jnp.concatenate([grad, hess], axis=0).reshape(2 * outputs, chunks, LANES)
    both = jnp.transpose(both, (1, 0, 2)).reshape(chunks * 2 * outputs, LANES)
    node = leaf.astype(jnp.bfloat16).reshape(chunks, LANES)
    node = jnp.pad(node, ((0, -chunks % 16), (0, 0)))
    packed = jnp.concatenate([both, node], axis=0)
    dma = pltpu.SemaphoreType.DMA((count,))
    gains, best = pl.pallas_call(
        functools.partial(kernel, sizes, outputs, shard, owned),
        out_shape=(
            jax.ShapeDtypeStruct((owned, LEAVES, B), jnp.float32),
            jax.ShapeDtypeStruct((1, LANES), jnp.float32),
        ),
        in_specs=[pl.BlockSpec(memory_space=pltpu.VMEM)] * 2,
        out_specs=(pl.BlockSpec(memory_space=pltpu.VMEM),) * 2,
        scratch_shapes=[
            pltpu.VMEM(codes.shape, jnp.bfloat16),
            pltpu.VMEM((count,) + packed.shape, jnp.bfloat16),
            pltpu.VMEM((owned, LEAVES * 2 * outputs, B), jnp.float32),
            pltpu.VMEM((count, 1, LANES), jnp.float32),
            dma, dma, dma, dma, dma, dma,
        ],
        compiler_params=pltpu.CompilerParams(
            collective_id=0, has_side_effects=True, vmem_limit_bytes=56 * 1024 * 1024
        ),
    )(codes, packed)
    return gains, best[0, ::LANES // LEAVES]


def solution(mesh):
    rows, feat = mesh.shape["rows"], mesh.shape["feat"]
    sizes = (rows // 2, 2, feat // 2)
    return jax.shard_map(
        functools.partial(shards, sizes),
        mesh=mesh,
        in_specs=(
            P(None, ("rows", "feat")),
            P(("rows", "feat")),
            P(None, ("rows", "feat")),
            P(None, ("rows", "feat")),
        ),
        out_specs=(P(("rows", "feat"), None, None), P()),
        check_vma=False,
    )
```

time: 227 us -> 88.6 us (0.39)
  blocking collectives: 140 us -> 0 us
  Pallas kernels: 0 us -> 80.7 us
  matrix products: 52.4 us -> 0 us
  between operations: 14.1 us -> 0.65 us
  starting transfers between devices: 7.37 us -> 0 us
  local copies, waits for them, and re-layouts: 8.17 us -> 2.55 us
    pallas_call x0 -> x1, Pallas kernels: none -> 80.7 us  [shards(): pl.pallas_call(functools.partial(kernel, sizes, outputs, shard, owned), o...]
    all_gather x1 -> x0, blocking collectives: 60.4 us -> none  [shards(): lax.all_gather(leaf_row.astype(jnp.bfloat16), ('rows', 'feat'), axis=1, t...]
    dot_general x4 -> x0, matrix products: 52.4 us -> none  [bin_counts(): jnp.einsum('frb,cr->fbc', onehot, weighted, preferred_element_type=jnp.fl...]
    pmax x1 -> x0, blocking collectives: 41.8 us -> none  [shards(): best = lax.pmax(jnp.max(gains, axis=(0, 2)), ('rows', 'feat'))]
    psum x1 -> x0, blocking collectives: 37.5 us -> none  [shards(): lax.psum(jnp.sum(weighted, axis=1, dtype=jnp.float32), ('rows', 'feat'))]
    all_to_all x1 -> x0, starting transfers between devices: 7.33 us -> none  [shards(): lax.all_to_all(bins, ('rows', 'feat'), split_axis=0, concat_axis=1, tiled...]
    dynamic_slice x8 -> x0, local copies, waits for them, and re-layouts: 5.28 us -> none  [the longest x4 5.17 us: step(): part_both = lax.dynamic_slice_in_dim(both_piece, offset, width, 1)]
    reshape x0 -> x3, other arithmetic: none -> 3.68 us  [the longest x1 2.09 us: shards(): codes = bins.astype(jnp.bfloat16).reshape(count, owned, shard)]
  transfers between devices with their start and end apart: 2 -> 0, of which waited for: 0 -> 0; matrix products, arithmetic and copies ran while one was open for 0% -> 0% of each run, Pallas kernels for 0% -> 0%
where the time goes in v1:
time: 88.6 us; the launch traced here: 88.2 us
  Pallas kernels  80.7 us (91%)
  other arithmetic  4.34 us (5%)
  local copies, waits for them, and re-layouts  2.55 us (3%)
    pallas_call x1, Pallas kernels, shards(): pl.pallas_call(functools.partial(kernel, sizes, outputs, shard, owned), o...  80.7 us
    reshape x1, other arithmetic, shards(): codes = bins.astype(jnp.bfloat16).reshape(count, owned, shard)  2.09 us
    unnamed x3, local copies, waits for them, and re-layouts  1.95 us

profile of v1, /device:TPU:0, one launch (start us, length us, event | category | flops | bytes accessed | tf_op | source)
XLA Modules:
  0.0 88.2 jit_solution(1066824470918238115)
XLA Ops:
  0.6 0.7 convert_bitcast_fusion.1
  1.3 0.9 %copy_bitcast_fusion = bf16[64,8,128]{2,0,1:T(8,128)(2,1)S(1)} fusion(bf16[32,1024]{1,0:T(8,128)(2,1)} %param.7, bf16[32,1024]{1,0:T(8,128)(2,1)} %param.6), kind=kLoop, calls=%fused_computation.4 | loop fusion | flops 262144 | bytes 262144 | tf_op jit(solution)/shard_map/reshape | solution.py:202
  2.2 0.7 fusion.1.packed_in
  2.9 2.1 %convert_bitcast_fusion.codes_in = bf16[32,8,1024]{2,1,0:T(8,128)(2,1)} fusion(s32[256,1024]{1,0:T(8,128)} %param.4), kind=kLoop, calls=%fused_computation | loop fusion | flops 262144 | bytes 1572864 | tf_op jit(solution)/shard_map/reshape | solution.py:201
  5.0 80.7 %shard_map.59 = (f32[8,2,256]{2,1,0:T(2,128)}, f32[1,128]{1,0:T(1,128)}) custom-call(bf16[32,8,1024]{2,1,0:T(8,128)(2,1)} %convert_bitcast_fusion.codes_in, bf16[528,128]{1,0:T(8,128)(2,1)} %fusion.1.packed_in), custom_call_target="tpu_custom_call" | custom-call | tf_op jit(solution)/shard_map/pallas_call | solution.py:208
  85.7 0.0 copy-start
  85.7 0.6 copy-done
  86.3 0.6 slice.3
  86.9 1.3 %copy.10 = f32[8,2,256]{2,1,0:T(2,128)} copy(f32[8,2,256]{2,1,0:T(2,128)} %get-tuple-element.8) | data formatting | bytes 32768
Async XLA Ops:
  85.7 0.6 copy-start

commit v2 on v1

v2 whole, which is shorter than its diff:
```python
import functools

import jax
import jax.numpy as jnp
from jax import lax
from jax.experimental import pallas as pl
from jax.experimental.pallas import tpu as pltpu
from jax.sharding import PartitionSpec as P

B = 256
LEAVES = 2
LANES = 128
MESH = pl.DeviceIdType.MESH


def add_block(codes, packed, acc_ref, outputs, shard):
    chunks = shard // LANES
    height = 2 * outputs
    both = jnp.concatenate([packed[j * height:(j + 1) * height, :] for j in range(chunks)], axis=1)
    start = chunks * height
    node = jnp.concatenate([packed[start + j:start + j + 1, :] for j in range(chunks)], axis=1)
    zero = jnp.zeros_like(both)
    weighted = jnp.concatenate([jnp.where(node == leaf, both, zero) for leaf in range(LEAVES)], axis=0)
    columns = codes.astype(jnp.float32).T.astype(jnp.bfloat16)
    levels = lax.broadcasted_iota(jnp.int32, (shard, B), 1).astype(jnp.float32).astype(jnp.bfloat16)
    one = jnp.ones((shard, B), jnp.bfloat16)
    none = jnp.zeros((shard, B), jnp.bfloat16)
    for f in range(codes.shape[0]):
        code = jnp.broadcast_to(columns[:, f:f + 1], (shard, B))
        acc_ref[f] += jnp.dot(weighted, jnp.where(code <= levels, one, none), preferred_element_type=jnp.float32)


def feature_gains(cum, outputs):
    rows = []
    for leaf in range(LEAVES):
        base = leaf * 2 * outputs
        left_grad = cum[base:base + outputs]
        left_hess = cum[base + outputs:base + 2 * outputs]
        all_grad = left_grad[:, B - 1:B]
        all_hess = left_hess[:, B - 1:B]
        right_grad = all_grad - left_grad
        right_hess = all_hess - left_hess
        score = (
            left_grad * left_grad / (left_hess + 1.0)
            + right_grad * right_grad / (right_hess + 1.0)
            - all_grad * all_grad / (all_hess + 1.0)
        )
        rows.append(0.5 / outputs * jnp.sum(score, axis=0, keepdims=True))
    return jnp.concatenate(rows, axis=0)


def kernel(sizes, outputs, shard, owned, bins_ref, leaf_ref, grad_ref, hess_ref, gains_ref, best_ref,
           codes_in, codes_all, packed_all, acc_ref, best_all, send_c, recv_c, send_g, recv_g, send_b, recv_b):
    na, nb, nz = sizes
    pairs = na * nb * nz
    count = 2 * pairs
    r = lax.axis_index("rows")
    f = lax.axis_index("feat")
    a, b = r // nb, r % nb
    z, c = f // 2, f % 2

    group = na * nb

    def place(pa, pb, pz, pc):
        return {"rows": pa * nb + pb, "feat": pz * 2 + pc}

    def line(pa, pb, pz, pc):
        return ((pa * nb + pb) * nz + pz) * 2 + pc

    def toggled(dz):
        value, bit = 0, 1
        while bit < nz:
            value = value + (z // bit + dz // bit) % 2 * bit
            bit *= 2
        return value

    def offsets(p, pc):
        da = (1 - pc) * ((p // nb) % na) + pc * (p % na)
        db = (1 - pc) * (p % nb) + pc * ((p // na) % nb)
        return da, db, p // group

    me = line(a, b, z, c)
    other = 1 - c

    def source(p, pc):
        da, db, dz = offsets(p, pc)
        return line((a + da) % na, (b + db) % nb, toggled(dz), pc)

    def target(s):
        da, db, dz = offsets(s // 2, c)
        return (a + na - da) % na, (b + nb - db) % nb, toggled(dz), (c + s) % 2

    rows_size, feat_size = na * nb, nz * 2
    row_at = [lax.rem(r + i, rows_size) for i in range(rows_size)]
    feat_at = [lax.rem(f + i, feat_size) for i in range(feat_size)]
    others = [(i, j) for i in range(rows_size) for j in range(feat_size) if i + j > 0]

    barrier = pltpu.get_barrier_semaphore()
    for i, j in others:
        pl.semaphore_signal(
            barrier, inc=1, device_id={"rows": row_at[i], "feat": feat_at[j]}, device_id_type=MESH)

    chunks = shard // LANES
    own = packed_all.at[me]
    for j in range(chunks):
        part = slice(j * LANES, (j + 1) * LANES)
        own[2 * j * outputs:(2 * j + 1) * outputs] = grad_ref[:, part]
        own[(2 * j + 1) * outputs:(2 * j + 2) * outputs] = hess_ref[:, part]
    node = leaf_ref[...].astype(jnp.float32)
    node = jnp.concatenate([node, jnp.zeros((-chunks % 16, LANES), jnp.float32)], axis=0)
    own[2 * chunks * outputs:] = node.astype(jnp.bfloat16)
    codes_in[...] = bins_ref[...].astype(jnp.float32).astype(jnp.bfloat16).reshape(codes_in.shape)
    codes_all[me] = codes_in[me]
    acc_ref[...] = jnp.zeros_like(acc_ref)

    pl.semaphore_wait(barrier, count - 1)

    def packed_copy(src, slot, sem, where):
        return pltpu.make_async_remote_copy(
            src_ref=src, dst_ref=packed_all.at[slot], send_sem=send_g.at[sem], recv_sem=recv_g.at[slot],
            device_id=where, device_id_type=MESH)

    def codes_copy(s):
        where = target(s)
        return pltpu.make_async_remote_copy(
            src_ref=codes_in.at[line(*where)], dst_ref=codes_all.at[me], send_sem=send_c.at[s],
            recv_sem=recv_c.at[me], device_id=place(*where), device_id_type=MESH)

    def best_copy(i, j):
        return pltpu.make_async_remote_copy(
            src_ref=best_all.at[me], dst_ref=best_all.at[me], send_sem=send_b.at[i * feat_size + j],
            recv_sem=recv_b.at[me], device_id={"rows": row_at[i], "feat": feat_at[j]}, device_id_type=MESH)

    def forward(p, block, slot):
        for core in range(2):
            n1, n2 = (nb, na) if core == 0 else (na, nb)

            def spot(step, k):
                along_b = (step == 1) == (core == 0)
                if along_b:
                    return place(a, (b + nb - k) % nb, z, c)
                return place((a + na - k) % na, b, z, c)

            @pl.when(jnp.logical_and(c == core, (p // n1) % n2 == 0))
            def _():
                for k in range(1, n2):
                    sem = nz * n1 + (p // group * n1 + p % n1) * (n2 - 1) + k - 1
                    packed_copy(block, slot, sem, spot(2, k)).start()

            @pl.when(jnp.logical_and(c == core, p % group == 0))
            def _():
                for k in range(1, n1):
                    packed_copy(block, slot, nz + p // group * (n1 - 1) + k - 1, spot(1, k)).start()

        packed_copy(block, slot, nz * group + p, place(a, b, z, other)).start()

    def take(p):
        slot = source(p, c)
        packed_copy(own, slot, 0, place(a, b, z, other)).wait_recv()
        forward(p, packed_all.at[slot], slot)

    for k in range(1, nz):
        packed_copy(own, me, k, place(a, b, toggled(k), c)).start()
    forward(jnp.int32(0), own, me)

    @pl.loop(1, count)
    def _(s):
        codes_copy(s).start()

    @pl.loop(0, count)
    def _(s):
        p = s // 2
        here = source(p, (c + s) % 2)

        @pl.when(s > 0)
        def _():
            codes_copy_wait = pltpu.make_async_remote_copy(
                src_ref=codes_all.at[here], dst_ref=codes_all.at[here], send_sem=send_c.at[0],
                recv_sem=recv_c.at[here], device_id=place(a, b, z, other), device_id_type=MESH)
            codes_copy_wait.wait_recv()

        @pl.when(s % 2 == 1)
        def _():
            packed_copy(own, here, 0, place(a, b, z, other)).wait_recv()

        add_block(codes_all[here], packed_all[here], acc_ref, outputs, shard)

        @pl.when(jnp.logical_and(s % 2 == 0, jnp.logical_and((p + 1) % group > 0, s + 2 < count)))
        def _():
            take(p + 1)

        @pl.when(jnp.logical_and(s % 2 == 0, jnp.logical_and(p % group == 1, p // group + 1 < nz)))
        def _():
            take((p // group + 1) * group)

    top = None
    for i in range(owned):
        value = feature_gains(acc_ref[i], outputs)
        gains_ref[i] = value
        top = value if top is None else jnp.maximum(top, value)
    peak = jnp.max(top, axis=1, keepdims=True)
    lane = lax.broadcasted_iota(jnp.int32, (1, LANES), 1)
    best_all[me] = jnp.where(lane < LANES // 2, peak[0:1], peak[1:2])

    @pl.loop(1, count)
    def _(s):
        pltpu.make_async_remote_copy(
            src_ref=codes_in.at[0], dst_ref=codes_all.at[0], send_sem=send_c.at[s],
            recv_sem=recv_c.at[0], device_id=place(a, b, z, other), device_id_type=MESH).wait_send()
        packed_copy(own, me, s, place(a, b, z, other)).wait_send()

    for i, j in others:
        best_copy(i, j).start()

    @pl.loop(0, count)
    def _(here):
        @pl.when(here != me)
        def _():
            pltpu.make_async_remote_copy(
                src_ref=best_all.at[here], dst_ref=best_all.at[here], send_sem=send_b.at[0],
                recv_sem=recv_b.at[here], device_id=place(a, b, z, other), device_id_type=MESH).wait_recv()

    for i, j in others:
        best_copy(i, j).wait_send()

    best_ref[...] = jnp.max(best_all[...], axis=0)


def shards(sizes, bins, leaf, grad, hess):
    na, nb, nz = sizes
    count = na * nb * nz * 2
    outputs = grad.shape[0]
    features, shard = bins.shape
    owned = features // count
    chunks = shard // LANES
    packed_rows = chunks * 2 * outputs + chunks + -chunks % 16
    codes_shape = (count, owned, shard)
    dma = pltpu.SemaphoreType.DMA((count,))
    gains, best = pl.pallas_call(
        functools.partial(kernel, sizes, outputs, shard, owned),
        out_shape=(
            jax.ShapeDtypeStruct((owned, LEAVES, B), jnp.float32),
            jax.ShapeDtypeStruct((1, LANES), jnp.float32),
        ),
        in_specs=[pl.BlockSpec(memory_space=pltpu.VMEM)] * 4,
        out_specs=(pl.BlockSpec(memory_space=pltpu.VMEM),) * 2,
        scratch_shapes=[
            pltpu.VMEM(codes_shape, jnp.bfloat16),
            pltpu.VMEM(codes_shape, jnp.bfloat16),
            pltpu.VMEM((count, packed_rows, LANES), jnp.bfloat16),
            pltpu.VMEM((owned, LEAVES * 2 * outputs, B), jnp.float32),
            pltpu.VMEM((count, 1, LANES), jnp.float32),
            dma, dma, dma, dma, dma, dma,
        ],
        compiler_params=pltpu.CompilerParams(
            collective_id=0, has_side_effects=True, vmem_limit_bytes=56 * 1024 * 1024
        ),
    )(bins, leaf.reshape(chunks, LANES), grad, hess)
    return gains, best[0, ::LANES // LEAVES]


def solution(mesh):
    rows, feat = mesh.shape["rows"], mesh.shape["feat"]
    sizes = (rows // 2, 2, feat // 2)
    return jax.shard_map(
        functools.partial(shards, sizes),
        mesh=mesh,
        in_specs=(
            P(None, ("rows", "feat")),
            P(("rows", "feat")),
            P(None, ("rows", "feat")),
            P(None, ("rows", "feat")),
        ),
        out_specs=(P(("rows", "feat"), None, None), P()),
        check_vma=False,
    )
```

time: 88.6 us -> 60.6 us (0.68)
  Pallas kernels: 80.7 us -> 57.2 us
  other arithmetic: 4.34 us -> 0 us
    pallas_call x1, Pallas kernels: 80.7 us -> 57.2 us  [shards(): pl.pallas_call(functools.partial(kernel, sizes, outputs, shard, owned), o...]
    reshape x3 -> x0, other arithmetic: 3.68 us -> none  [the longest x1 2.09 us: shards(): codes = bins.astype(jnp.bfloat16).reshape(count, owned, shard)]
where the time goes in v2:
time: 60.6 us; the launch traced here: 60.4 us
  Pallas kernels  57.2 us (94%)
  local copies, waits for them, and re-layouts  2.58 us (4%)
  between operations  0.65 us (1%)
    pallas_call x1, Pallas kernels, shards(): pl.pallas_call(functools.partial(kernel, sizes, outputs, shard, owned), o...  57.2 us
    unnamed x3, local copies, waits for them, and re-layouts  1.98 us

profile of v2, /device:TPU:0, one launch (start us, length us, event | category | flops | bytes accessed | tf_op | source)
XLA Modules:
  0.0 60.4 jit_solution(17654932018385054194)
XLA Ops:
  0.6 57.2 %shard_map.59 = (f32[8,2,256]{2,1,0:T(2,128)}, f32[1,128]{1,0:T(1,128)}) custom-call(s32[256,1024]{1,0:T(8,128)} %bins_ref.1, s32[8,128]{1,0:T(8,128)} %bitcast.2, bf16[32,1024]{1,0:T(8,128)(2,1)} %grad_ref.1, bf16[32,1024]{1,0:T(8,128)(2,1)} %hess_ref.1), custom_call_target="tpu_custom_call" | custom-call | tf_op jit(solution)/shard_map/pallas_call | solution.py:239
  57.8 0.0 copy-start
  57.8 0.7 %copy-done = f32[1,128]{1,0:T(1,128)S(1)} copy-done((f32[1,128]{1,0:T(1,128)S(1)}, f32[1,128]{1,0:T(1,128)}, u32[]{:S(2)}) %copy-start) | copy-done | bytes 536
  58.5 0.6 slice.3
  59.1 1.3 %copy.7 = f32[8,2,256]{2,1,0:T(2,128)} copy(f32[8,2,256]{2,1,0:T(2,128)} %get-tuple-element.8) | data formatting | bytes 32768
Async XLA Ops:
  57.8 0.7 %copy-start = (f32[1,128]{1,0:T(1,128)S(1)}, f32[1,128]{1,0:T(1,128)}, u32[]{:S(2)}) copy-start(f32[1,128]{1,0:T(1,128)} %get-tuple-element.5) | copy-start | bytes 1540

commit v3 on v2

--- a/solution.py
+++ b/solution.py
@@ -163,8 +163,7 @@
         packed_copy(own, me, k, place(a, b, toggled(k), c)).start()
     forward(jnp.int32(0), own, me)
 
-    @pl.loop(1, count)
-    def _(s):
+    for s in range(1, count):
         codes_copy(s).start()
 
     @pl.loop(0, count)

time: 60.6 us -> 60.4 us (level)
  no operation moved by 1% of the time
where the time goes in v3:
time: 60.4 us; the launch traced here: 60.1 us
  Pallas kernels  56.9 us (94%)
  local copies, waits for them, and re-layouts  2.58 us (4%)
  between operations  0.65 us (1%)
    pallas_call x1, Pallas kernels, shards(): pl.pallas_call(functools.partial(kernel, sizes, outputs, shard, owned), o...  56.9 us
    unnamed x3, local copies, waits for them, and re-layouts  1.98 us

profile of v3, /device:TPU:0, one launch (start us, length us, event | category | flops | bytes accessed | tf_op | source)
XLA Modules:
  0.0 60.1 jit_solution(8962267901280215750)
XLA Ops:
  0.6 56.9 %shard_map.59 = (f32[8,2,256]{2,1,0:T(2,128)}, f32[1,128]{1,0:T(1,128)}) custom-call(s32[256,1024]{1,0:T(8,128)} %bins_ref.1, s32[8,128]{1,0:T(8,128)} %bitcast.2, bf16[32,1024]{1,0:T(8,128)(2,1)} %grad_ref.1, bf16[32,1024]{1,0:T(8,128)(2,1)} %hess_ref.1), custom_call_target="tpu_custom_call" | custom-call | tf_op jit(solution)/shard_map/pallas_call | solution.py:238
  57.5 0.0 copy-start
  57.6 0.7 %copy-done = f32[1,128]{1,0:T(1,128)S(1)} copy-done((f32[1,128]{1,0:T(1,128)S(1)}, f32[1,128]{1,0:T(1,128)}, u32[]{:S(2)}) %copy-start) | copy-done | bytes 536
  58.2 0.6 slice.3
  58.8 1.3 %copy.7 = f32[8,2,256]{2,1,0:T(2,128)} copy(f32[8,2,256]{2,1,0:T(2,128)} %get-tuple-element.8) | data formatting | bytes 32768
Async XLA Ops:
  57.5 0.7 %copy-start = (f32[1,128]{1,0:T(1,128)S(1)}, f32[1,128]{1,0:T(1,128)}, u32[]{:S(2)}) copy-start(f32[1,128]{1,0:T(1,128)} %get-tuple-element.5) | copy-start | bytes 1540
